TPU v7x, 256 devices: a whole 4x4x8 slice. The times are simulated.
256 devices in a mesh: trial: 4 (over x_lo, core), north: 16 (over z_hi, y, x_hi), east: 4 (over z_lo).
Axes of the slice: x: 4 (x_hi: 2, x_lo: 2; x = x_hi * 2 + x_lo), y: 4, z: 8 (z_hi: 2, z_lo: 4; z = z_hi * 4 + z_lo), core: 2. Of those that a mesh axis runs over, the one named last changes fastest.
Arguments:
- pair_state: bfloat16 [1536, 384, 128], P(('trial', 'north'), 'east'), parts along dimension 0, may hold values from -6 to 6
- in_gain: float32 [128], replicated, may hold values from 0.25 to 1.75
- left_weight: bfloat16 [512, 128], P('trial'), parts along dimension 0, may hold values from -0.5 to 0.5
- right_weight: bfloat16 [512, 128], P('trial'), parts along dimension 0, may hold values from -0.5 to 0.5
- left_gate: bfloat16 [512, 128], P('trial'), parts along dimension 0, may hold values from -0.5 to 0.5
- right_gate: bfloat16 [512, 128], P('trial'), parts along dimension 0, may hold values from -0.5 to 0.5
- mid_gain: float32 [128], replicated, may hold values from 0.25 to 1.75
- out_weight: bfloat16 [512, 128], P('trial'), parts along dimension 0, may hold values from -0.5 to 0.5
- out_gate: bfloat16 [512, 128], P('trial'), parts along dimension 0, may hold values from -0.5 to 0.5
Outputs:
- triangle_out: bfloat16 [1536, 384, 128], P(('trial', 'north'), 'east'), parts along dimension 0
There are 4 independent parts, one for each index of `trial`. A program takes and returns all parts, laid end to end along the dimension named above; an argument that names none is the same for every part. Nothing has to cross between parts.
All inputs are finite; a program needn't handle non-finite values.
Results may differ from a plain program's by a relative error of at most 0.015.
Values may be sent and summed in bfloat16 or wider, within the bound.
A program may use at most 64 MiB of HBM per device.

v0:
```python
import jax
import jax.numpy as jnp
from jax import lax
from jax.sharding import PartitionSpec as P


def norm_channels(values, channel_gain):
    centred = values - jnp.mean(values, axis=-1, keepdims=True)
    return (
        centred
        * lax.rsqrt(jnp.mean(centred * centred, axis=-1, keepdims=True) + 1e-05)
        * channel_gain
    )


def make_factors(pair_in, in_gain, left_weight, right_weight, left_gate, right_gate):
    ready = norm_channels(pair_in.astype(jnp.float32), in_gain).astype(jnp.bfloat16)
    ready = lax.optimization_barrier(ready)
    left = jnp.einsum("ijc,cd->ijd", ready, left_weight, preferred_element_type=jnp.float32)
    left = left * jax.nn.sigmoid(
        jnp.einsum("ijc,cd->ijd", ready, left_gate, preferred_element_type=jnp.float32)
    )
    right = jnp.einsum("ijc,cd->ijd", ready, right_weight, preferred_element_type=jnp.float32)
    right = right * jax.nn.sigmoid(
        jnp.einsum("ijc,cd->ijd", ready, right_gate, preferred_element_type=jnp.float32)
    )
    return (ready, left.astype(jnp.bfloat16), right.astype(jnp.bfloat16))


def to_pair(mixed, ready, mid_gain, out_weight, out_gate):
    scaled = norm_channels(mixed.astype(jnp.float32), mid_gain).astype(jnp.bfloat16)
    scaled = lax.optimization_barrier(scaled)
    gate = jax.nn.sigmoid(
        jnp.einsum("ijc,cd->ijd", ready, out_gate, preferred_element_type=jnp.float32)
    )
    return (
        jnp.einsum("ijd,dc->ijc", scaled, out_weight, preferred_element_type=jnp.float32) * gate
    ).astype(jnp.bfloat16)


def local(
    pair_state,
    in_gain,
    left_weight,
    right_weight,
    left_gate,
    right_gate,
    mid_gain,
    out_weight,
    out_gate,
):
    ready, left, right = make_factors(
        pair_state, in_gain, left_weight, right_weight, left_gate, right_gate
    )
    count = pair_state.shape[1] * lax.axis_size("east")
    left_lines, right_lines = (
        lax.all_to_all(left, "east", split_axis=2, concat_axis=1, tiled=True),
        lax.all_to_all(right, "east", split_axis=2, concat_axis=1, tiled=True),
    )
    strip = jnp.einsum(
        "ikd,jkd->ijd",
        left_lines,
        lax.all_gather(right_lines, "north", axis=0, tiled=True),
        preferred_element_type=jnp.float32,
    )
    strip = (strip * count ** (-0.5)).astype(jnp.bfloat16)
    mixed = lax.all_to_all(strip, "east", split_axis=1, concat_axis=2, tiled=True)
    return to_pair(mixed, ready, mid_gain, out_weight, out_gate)


def solution(mesh):
    return jax.shard_map(
        local,
        mesh=mesh,
        in_specs=(
            P(("trial", "north"), "east", None),
            P(),
            P("trial", None),
            P("trial", None),
            P("trial", None),
            P("trial", None),
            P(),
            P("trial", None),
            P("trial", None),
        ),
        out_specs=P(("trial", "north"), "east", None),
        check_vma=False,
    )
```

profile of v0, /device:TPU:8, one launch (start us, length us, event | category | flops | bytes accessed | tf_op | source)
XLA Modules:
  0.0 274.5 jit_solution(15946560418342138973)
XLA Ops:
  6.5 0.0 copy-start
  6.5 0.0 copy-start.1
  6.5 0.0 copy-start.5
  6.5 0.0 all-gather.2.cloned.1.call-start
  6.5 1.4 convert_reduce_fusion
  8.0 1.9 fusion.21
  9.9 0.0 copy-done.1
  9.9 0.0 copy-done.5
  9.9 0.8 fusion.23
  10.7 0.0 copy-done
  10.7 0.0 copy-start.2
  10.7 0.5 fusion.15
  11.2 0.3 copy-done.2
  11.5 0.3 fusion.16
  11.8 0.4 copy.28
  12.2 25.8 %all_to_all.45 = bf16[24,96,128]{1,0,2:T(8,128)(2,1)S(1)} all-to-all(bf16[24,96,128]{1,0,2:T(8,128)(2,1)S(1)} %copy.28), channel_id=1, replica_groups=mesh['trial'=4,'north'=16,'east'=4] {'east'}, dimensions={2} | all-to-all | bytes 1179648 | tf_op jit(solution)/shard_map/all_to_all | solution.py:58
  38.0 0.6 copy.30
  38.6 0.0 copy-start.7
  38.6 1.3 all_to_all.36
  40.0 0.0 all-gather.2.cloned.1.call-update
  40.0 0.0 copy-done.7
  40.0 0.0 copy-start.3
  40.0 0.5 fusion.12
  40.5 0.3 copy-done.3
  40.8 0.3 fusion.17
  41.1 0.4 copy.31
  41.5 30.6 %all_to_all.46 = bf16[24,96,128]{1,0,2:T(8,128)(2,1)S(1)} all-to-all(bf16[24,96,128]{1,0,2:T(8,128)(2,1)S(1)} %copy.31), channel_id=1, replica_groups=mesh['trial'=4,'north'=16,'east'=4] {'east'}, dimensions={2} | all-to-all | bytes 1179648 | tf_op jit(solution)/shard_map/all_to_all | solution.py:57
  72.1 0.6 copy.33
  72.8 0.5 all_to_all.40
  73.3 153.3 %all-gather.2.cloned.1.call-done = bf16[384,384,32]{1,0,2:T(8,128)(2,1)} async-done(((bf16[24,384,32]{1,0,2:T(8,128)(2,1)}), bf16[384,384,32]{1,0,2:T(8,128)(2,1)}) %all-gather.2.cloned.1.call-update) | async-done | bytes 9437200 | tf_op jit(solution)/shard_map/all_gather | solution.py:63
  226.6 7.9 %fusion.20 = bf16[24,384,32]{1,0,2:T(8,128)(2,1)} fusion(bf16[384,384,32]{1,0,2:T(8,128)(2,1)} %all-gather.2.cloned.1.call-done, bf16[24,384,32]{1,0,2:T(8,128)(2,1)S(1)} %all_to_all.40), kind=kOutput, calls=%fused_computation.32 | convolution fusion | flops 227082240 | bytes 10616832 | tf_op jit(solution)/shard_map/ikd,jkd->ijd/dot_general | solution.py:60
  234.4 3.0 %copy.34 = bf16[24,384,32]{2,0,1:T(8,128)(2,1)S(1)} copy(bf16[24,384,32]{1,0,2:T(8,128)(2,1)} %fusion.20) | data formatting | bytes 1179648 | tf_op jit(solution)/shard_map/convert_element_type | solution.py:66
  237.5 3.1 %reshape.41 = bf16[4,2,36864]{2,1,0:T(2,128)(2,1)} reshape(bf16[384,24,32]{2,1,0:T(8,128)(2,1)S(1)} %bitcast.58) | data formatting | bytes 1179648
  240.6 0.0 copy-start.8
  240.6 3.6 %all-to-all-start.2 = ((bf16[4,2,36864]{2,1,0:T(2,128)(2,1)}), bf16[4,2,36864]{2,1,0:T(2,128)(2,1)S(1)}, u32[]{:S(2)}, u32[]{:S(2)}) async-start(bf16[4,2,36864]{2,1,0:T(2,128)(2,1)} %reshape.41), calls=%async_computation.2 | async-start | bytes 1179648 | tf_op jit(solution)/shard_map/all_to_all | solution.py:67
  244.2 0.0 copy-done.8
  244.3 0.5 fusion.9
  244.7 14.9 %all-to-all-done.2 = bf16[4,2,36864]{2,1,0:T(2,128)(2,1)S(1)} async-done(((bf16[4,2,36864]{2,1,0:T(2,128)(2,1)}), bf16[4,2,36864]{2,1,0:T(2,128)(2,1)S(1)}, u32[]{:S(2)}, u32[]{:S(2)}) %all-to-all-start.2) | async-done | bytes 589856 | tf_op jit(solution)/shard_map/all_to_all | solution.py:67
  259.6 2.5 reshape.42
  262.1 2.7 copy.35
  264.8 0.2 bitcast_reduce_fusion
  265.0 0.0 copy-start.6
  265.1 0.2 fusion.4
  265.3 0.4 copy-done.6
  265.7 0.0 copy-start.4
  265.7 0.3 fusion.2
  266.0 0.4 copy-done.4
  266.5 1.2 fusion.18
  (4 shorter events, 0.0 us)
Async XLA Ops:
  6.5 4.2 %copy-start = (bf16[128,128]{1,0:T(8,128)(2,1)S(1)}, bf16[128,128]{1,0:T(8,128)(2,1)}, u32[]{:S(2)}) copy-start(bf16[128,128]{1,0:T(8,128)(2,1)} %param.14) | copy-start | bytes 98308
  6.5 3.3 %copy-start.1 = (bf16[24,96,128]{2,1,0:T(8,128)(2,1)S(1)}, bf16[24,96,128]{2,1,0:T(8,128)(2,1)}, u32[]{:S(2)}) copy-start(bf16[24,96,128]{2,1,0:T(8,128)(2,1)} %param.9) | copy-start | bytes 1769476
  6.5 3.3 %copy-start.5 = (f32[128]{0:T(128)S(1)}, f32[128]{0:T(128)}, u32[]{:S(2)}) copy-start(f32[128]{0:T(128)} %param.10) | copy-start | bytes 1540
  6.5 220.0 %all-gather.2.cloned.1.call-start = ((), (), s32[]{:S(2)}) async-start(), calls=%async_computation.3 | async-start | bytes 10027008 | tf_op jit(solution)/shard_map/all_gather | solution.py:63
  10.7 0.8 copy-start.2
  38.6 1.4 copy-start.7
  40.0 0.8 copy-start.3
  240.6 3.6 %copy-start.8 = (bf16[128,128]{1,0:T(8,128)(2,1)S(1)}, bf16[128,128]{1,0:T(8,128)(2,1)}, u32[]{:S(2)}) copy-start(bf16[128,128]{1,0:T(8,128)(2,1)} %param.17) | copy-start | bytes 98308
  240.6 19.0 %all-to-all-start.2 = ((bf16[4,2,36864]{2,1,0:T(2,128)(2,1)}), bf16[4,2,36864]{2,1,0:T(2,128)(2,1)S(1)}, u32[]{:S(2)}, u32[]{:S(2)}) async-start(bf16[4,2,36864]{2,1,0:T(2,128)(2,1)} %reshape.41), calls=%async_computation.2 | async-start | bytes 1179648 | tf_op jit(solution)/shard_map/all_to_all | solution.py:67
  265.0 0.7 copy-start.6
  265.7 0.8 copy-start.4
Sparse Core Ops, SparseCore 0:
  40.1 186.3 all-gather.1
where the time goes:
time: 277 us; the launch traced here: 275 us
  waiting for transfers between devices  168 us (61%)
  blocking collectives  56.4 us (20%)
  local copies, waits for them, and re-layouts  16.7 us (6%)
  between operations  13.6 us (5%)
  matrix products  11.1 us (4%)
  other arithmetic  4.88 us (2%)
  starting transfers between devices  3.61 us (1%)
    all_gather x1, waiting for transfers between devices, local(): lax.all_gather(right_lines, 'north', axis=0, tiled=True)  153 us
    all_to_all x1, blocking collectives, local(): lax.all_to_all(left, 'east', split_axis=2, concat_axis=1, tiled=True)  30.6 us
    all_to_all x1, blocking collectives, local(): lax.all_to_all(right, 'east', split_axis=2, concat_axis=1, tiled=True)  25.8 us
    all_to_all x1, waiting for transfers between devices, local(): lax.all_to_all(strip, 'east', split_axis=1, concat_axis=2, tiled=True)  14.9 us
    dot_general x1, matrix products, local(): jnp.einsum('ikd,jkd->ijd', left_lines, lax.all_gather(right_lines, 'north...  7.89 us
    unnamed x20, local copies, waits for them, and re-layouts  7.02 us
  transfers between devices with their start and end apart: 2, of which 2 were waited for; matrix products, arithmetic and copies ran while one was open for 1% of the time, Pallas kernels for 0%

commit v1 on v0

v1 whole, which is shorter than its diff:
```python
import functools

import jax
import jax.numpy as jnp
from jax import lax
from jax.experimental import pallas as pl
from jax.experimental.pallas import tpu as pltpu
from jax.sharding import PartitionSpec as P

MESH = pl.DeviceIdType.MESH


def norm_channels(values, channel_gain, axis=-1):
    centred = values - jnp.mean(values, axis=axis, keepdims=True)
    return (
        centred
        * lax.rsqrt(jnp.mean(centred * centred, axis=axis, keepdims=True) + 1e-05)
        * channel_gain
    )


def exchange_kernel(north, east, src, dst, send_sem, recv_sem, own_sem):
    n = lax.axis_index("north")
    e = lax.axis_index("east")
    count = north * east
    me = n * east + e

    def peer(k):
        q = lax.rem(me + k, count)
        return q, {"north": q // east, "east": lax.rem(q, east)}

    barrier = pltpu.get_barrier_semaphore()

    def greet(k, carry):
        pl.semaphore_signal(barrier, inc=1, device_id=peer(k)[1], device_id_type=MESH)
        return carry

    lax.fori_loop(1, count, greet, 0)
    pl.semaphore_wait(barrier, count - 1)
    own = pltpu.make_async_copy(src.at[me], dst.at[me], own_sem)
    own.start()

    def send(k, carry):
        q, device = peer(k)
        pltpu.make_async_remote_copy(
            src_ref=src.at[q],
            dst_ref=dst.at[me],
            send_sem=send_sem,
            recv_sem=recv_sem,
            device_id=device,
            device_id_type=MESH,
        ).start()
        return carry

    lax.fori_loop(1, count, send, 0)
    own.wait()
    everything = pltpu.make_async_remote_copy(
        src_ref=src.at[pl.ds(0, count - 1)],
        dst_ref=dst.at[pl.ds(0, count - 1)],
        send_sem=send_sem,
        recv_sem=recv_sem,
        device_id={"north": n, "east": e},
        device_id_type=MESH,
    )
    everything.wait_recv()
    everything.wait_send()


def exchange(pieces, north, east, collective_id):
    return pl.pallas_call(
        functools.partial(exchange_kernel, north, east),
        out_shape=jax.ShapeDtypeStruct(pieces.shape, pieces.dtype),
        in_specs=[pl.BlockSpec(memory_space=pltpu.VMEM)],
        out_specs=pl.BlockSpec(memory_space=pltpu.VMEM),
        scratch_shapes=[
            pltpu.SemaphoreType.DMA,
            pltpu.SemaphoreType.DMA,
            pltpu.SemaphoreType.DMA,
        ],
        compiler_params=pltpu.CompilerParams(
            collective_id=collective_id, has_side_effects=True
        ),
    )(pieces)


def local(
    north,
    east,
    pair_state,
    in_gain,
    left_weight,
    right_weight,
    left_gate,
    right_gate,
    mid_gain,
    out_weight,
    out_gate,
):
    rows, cols, width = pair_state.shape
    group = north * east
    mix = left_weight.shape[1]
    own = mix // group
    ready = norm_channels(pair_state.astype(jnp.float32), in_gain).astype(jnp.bfloat16)
    ready = ready.reshape(rows * cols, width)

    def factor(weight, gate):
        value = jnp.einsum("pc,cd->dp", ready, weight, preferred_element_type=jnp.float32)
        value = value * jax.nn.sigmoid(
            jnp.einsum("pc,cd->dp", ready, gate, preferred_element_type=jnp.float32)
        )
        return value.astype(jnp.bfloat16).reshape(group, own, rows * cols)

    left = factor(left_weight, left_gate)
    right = factor(right_weight, right_gate)
    got = exchange(jnp.concatenate([left, right], axis=1), north, east, 0)
    got = got.reshape(north, east, 2, own, rows, cols).transpose(2, 3, 0, 4, 1, 5)
    got = got.reshape(2, own, north * rows, east * cols)
    mixed = jnp.einsum("dik,djk->dij", got[0], got[1], preferred_element_type=jnp.float32)
    mixed = (mixed * (east * cols) ** (-0.5)).astype(jnp.bfloat16)
    mixed = mixed.reshape(own, north, rows, east, cols).transpose(1, 3, 0, 2, 4)
    mixed = exchange(mixed.reshape(group, own, rows * cols), north, east, 1)
    mixed = mixed.reshape(mix, rows * cols)
    scaled = norm_channels(mixed.astype(jnp.float32), mid_gain[:, None], 0).astype(jnp.bfloat16)
    gate = jax.nn.sigmoid(
        jnp.einsum("pc,cd->pd", ready, out_gate, preferred_element_type=jnp.float32)
    )
    out = jnp.einsum("dp,dc->pc", scaled, out_weight, preferred_element_type=jnp.float32)
    return (out * gate).astype(jnp.bfloat16).reshape(rows, cols, width)


def solution(mesh):
    north, east = mesh.shape["north"], mesh.shape["east"]
    return jax.shard_map(
        functools.partial(local, north, east),
        mesh=mesh,
        in_specs=(
            P(("trial", "north"), "east", None),
            P(),
            P("trial", None),
            P("trial", None),
            P("trial", None),
            P("trial", None),
            P(),
            P("trial", None),
            P("trial", None),
        ),
        out_specs=P(("trial", "north"), "east", None),
        check_vma=False,
    )
```

time: 277 us -> 90.9 us (0.33)
  waiting for transfers between devices: 168 us -> 0 us
  Pallas kernels: 0 us -> 65.2 us
  blocking collectives: 56.4 us -> 0 us
  between operations: 13.6 us -> 0.28 us
  matrix products: 11.1 us -> 3.21 us
  local copies, waits for them, and re-layouts: 16.7 us -> 11.1 us
  other arithmetic: 4.88 us -> 9.83 us
  starting transfers between devices: 3.61 us -> 0 us
    all_gather x1 -> x0, waiting for transfers between devices: 153 us -> none  [local(): lax.all_gather(right_lines, 'north', axis=0, tiled=True)]
    pallas_call x0 -> x2, Pallas kernels: none -> 65.2 us  [exchange(): pl.pallas_call(functools.partial(exchange_kernel, north, east), out_shape...]
    all_to_all x2 -> x0, blocking collectives: 56.4 us -> none  [the longest x1 30.6 us: local(): lax.all_to_all(left, 'east', split_axis=2, concat_axis=1, tiled=True)]
    all_to_all x1 -> x0, waiting for transfers between devices: 14.9 us -> none  [local(): lax.all_to_all(strip, 'east', split_axis=1, concat_axis=2, tiled=True)]
    dot_general x7, matrix products: 11.1 us -> 3.21 us  [the longest x2 1.04 us: factor(): jnp.einsum('pc,cd->dp', ready, gate, preferred_element_type=jnp.float32)]
    reshape x0 -> x6, local copies, waits for them, and re-layouts: none -> 6.74 us  [the longest x1 3.65 us: local(): got.reshape(north, east, 2, own, rows, cols).transpose(2, 3, 0, 4, 1, 5)]
    unnamed x20, local copies, waits for them, and re-layouts: 7.02 us -> 1.22 us
    convert_element_type x4 -> x2, local copies, waits for them, and re-layouts: 6.59 us -> 1.22 us  [the longest x1 1.05 us: local(): return (out * gate).astype(jnp.bfloat16).reshape(rows, cols, width)]
  transfers between devices with their start and end apart: 2 -> 0, of which waited for: 2 -> 0; matrix products, arithmetic and copies ran while one was open for 1% -> 0% of each run, Pallas kernels for 0% -> 0%
where the time goes in v1:
time: 90.9 us; the launch traced here: 89.6 us
  Pallas kernels  65.2 us (72%)
  local copies, waits for them, and re-layouts  11.1 us (12%)
  other arithmetic  9.83 us (11%)
  matrix products  3.21 us (4%)
    pallas_call x2, Pallas kernels, exchange(): pl.pallas_call(functools.partial(exchange_kernel, north, east), out_shape...  65.2 us
    reduce_sum x2, other arithmetic, norm_channels(): jnp.mean(centred * centred, axis=axis, keepdims=True) + 1e-05  3.73 us
    reshape x1, local copies, waits for them, and re-layouts, local(): got.reshape(north, east, 2, own, rows, cols).transpose(2, 3, 0, 4, 1, 5)  3.65 us
    reduce_sum x2, other arithmetic, norm_channels(): centred = values - jnp.mean(values, axis=axis, keepdims=True)  3.03 us
    concatenate x1, other arithmetic, local(): got = exchange(jnp.concatenate([left, right], axis=1), north, east, 0)  2.23 us
    reshape x1, local copies, waits for them, and re-layouts, local(): mixed = exchange(mixed.reshape(group, own, rows * cols), north, east, 1)  1.91 us

profile of v1, /device:TPU:8, one launch (start us, length us, event | category | flops | bytes accessed | tf_op | source)
XLA Modules:
  0.0 89.6 jit_solution(5138245611772396420)
XLA Ops:
  0.0 0.0 copy-start
  0.0 0.0 copy-start.2
  0.0 0.0 copy-start.6
  0.0 1.4 %convert_reduce_fusion = f32[24,96]{1,0:T(8,128)S(1)} fusion(bf16[24,96,128]{2,1,0:T(8,128)(2,1)} %param.9), kind=kLoop, calls=%fused_computation.21 | loop fusion | flops 587520 | bytes 599040 | tf_op jit(solution)/shard_map/reduce_sum | solution.py:14
  1.4 1.9 %fusion.17 = f32[24,96]{1,0:T(8,128)S(1)} fusion(bf16[24,96,128]{2,1,0:T(8,128)(2,1)} %param.9, f32[24,96]{1,0:T(8,128)S(1)} %broadcast_multiply_fusion.1), kind=kLoop, calls=%fused_computation.26 | loop fusion | flops 1177344 | bytes 608256 | tf_op jit(solution)/shard_map/reduce_sum | solution.py:17
  3.3 0.0 copy-done.2
  3.3 0.0 copy-done.6
  3.4 0.8 fusion.19
  4.2 0.0 copy-done
  4.2 0.0 copy-start.3
  4.2 0.5 fusion.8
  4.7 0.2 copy-done.3
  5.0 0.4 fusion.13
  5.3 0.0 copy-start.8
  5.3 0.2 reshape.61
  5.6 0.5 copy-done.8
  6.1 0.0 copy-start.4
  6.1 0.5 fusion.5
  6.6 0.2 copy-done.4
  6.8 0.4 fusion.12
  7.2 0.2 reshape.62
  7.4 2.2 %pad_maximum_fusion.src = bf16[64,4,2304]{2,1,0:T(4,128)(2,1)} fusion(bf16[64,2,2304]{2,1,0:T(2,128)(2,1)S(1)} %reshape.62, bf16[64,2,2304]{2,1,0:T(2,128)(2,1)S(1)} %reshape.61), kind=kLoop, calls=%fused_computation.29 | loop fusion | flops 2359296 | bytes 2359296 | tf_op jit(solution)/shard_map/concatenate | solution.py:115
  9.7 40.9 %shard_map.91 = bf16[64,4,2304]{2,1,0:T(4,128)(2,1)} custom-call(bf16[64,4,2304]{2,1,0:T(4,128)(2,1)} %pad_maximum_fusion.src), custom_call_target="tpu_custom_call" | custom-call | tf_op jit(solution)/shard_map/pallas_call | solution.py:70
  50.6 3.6 %reshape.63 = bf16[16,4,2,2,24,96]{5,4,3,2,1,0:T(8,128)(2,1)S(1)} reshape(bf16[64,4,2304]{2,1,0:T(4,128)(2,1)} %shard_map.91) | data formatting | bytes 2359296 | tf_op jit(solution)/shard_map/reshape | solution.py:116
  54.3 0.3 fusion.23
  54.5 0.3 copy.16
  54.9 0.5 squeeze.6
  55.4 0.3 copy.17
  55.7 0.5 squeeze.7
  56.2 0.5 fusion.16
  56.8 0.6 reshape.64
  57.4 0.2 copy.25
  57.5 1.9 %reshape.65.src = bf16[64,2,2304]{2,1,0:T(2,128)(2,1)} reshape(bf16[16,4,2,24,96]{4,3,2,1,0:T(8,128)(2,1)S(1)} %bitcast.31) | data formatting | bytes 1179648 | tf_op jit(solution)/shard_map/reshape | solution.py:121
  59.4 24.2 %shard_map.92 = bf16[64,2,2304]{2,1,0:T(2,128)(2,1)} custom-call(bf16[64,2,2304]{2,1,0:T(2,128)(2,1)} %reshape.65.src), custom_call_target="tpu_custom_call" | custom-call | tf_op jit(solution)/shard_map/pallas_call | solution.py:70
  83.7 0.0 copy-start.1
  83.7 1.6 %convert_reduce_fusion.1 = f32[2304]{0:T(1024)S(1)} fusion(bf16[64,2,2304]{2,1,0:T(2,128)(2,1)} %shard_map.92), kind=kLoop, calls=%fused_computation.33 | loop fusion | flops 587520 | bytes 599040 | tf_op jit(solution)/shard_map/reduce_sum | solution.py:14
  85.3 0.0 copy-start.9
  85.3 1.9 %multiply_reduce_fusion = f32[2304]{0:T(1024)S(1)} fusion(bf16[64,2,2304]{2,1,0:T(2,128)(2,1)} %shard_map.92, f32[2304]{0:T(1024)S(1)} %broadcast_multiply_fusion), kind=kLoop, calls=%fused_computation.31 | loop fusion | flops 1177344 | bytes 608256 | tf_op jit(solution)/shard_map/reduce_sum | solution.py:17
  87.2 0.0 copy-done.1
  87.2 0.2 reshape.67
  87.4 0.0 copy-done.9
  87.4 0.0 copy-start.5
  87.4 0.0 copy-start.7
  87.4 0.5 fusion.2
  87.9 0.2 copy-done.5
  88.1 0.0 copy-done.7
  88.1 0.4 fusion.11
  88.5 1.1 %copy.21 = bf16[2304,128]{1,0:T(8,128)(2,1)} copy(bf16[2304,128]{0,1:T(8,128)(2,1)S(1)} %fusion.11) | data formatting | bytes 1179648 | tf_op jit(solution)/shard_map/convert_element_type | solution.py:128
  (4 shorter events, 0.0 us)
Async XLA Ops:
  0.0 4.2 %copy-start = (bf16[128,128]{1,0:T(8,128)(2,1)S(1)}, bf16[128,128]{1,0:T(8,128)(2,1)}, u32[]{:S(2)}) copy-start(bf16[128,128]{1,0:T(8,128)(2,1)} %param.13) | copy-start | bytes 98308
  0.0 3.3 %copy-start.2 = (bf16[24,96,128]{2,1,0:T(8,128)(2,1)S(1)}, bf16[24,96,128]{2,1,0:T(8,128)(2,1)}, u32[]{:S(2)}) copy-start(bf16[24,96,128]{2,1,0:T(8,128)(2,1)} %param.9) | copy-start | bytes 1769476
  0.0 3.3 %copy-start.6 = (f32[128]{0:T(128)S(1)}, f32[128]{0:T(128)}, u32[]{:S(2)}) copy-start(f32[128]{0:T(128)} %param.10) | copy-start | bytes 1540
  4.2 0.8 copy-start.3
  5.3 0.8 copy-start.8
  6.1 0.8 copy-start.4
  83.7 3.5 %copy-start.1 = (bf16[64,2,2304]{2,1,0:T(2,128)(2,1)S(1)}, bf16[64,2,2304]{2,1,0:T(2,128)(2,1)}, u32[]{:S(2)}) copy-start(bf16[64,2,2304]{2,1,0:T(2,128)(2,1)} %shard_map.92) | copy-start | bytes 1769476
  85.3 2.1 %copy-start.9 = (bf16[128,128]{1,0:T(8,128)(2,1)S(1)}, bf16[128,128]{1,0:T(8,128)(2,1)}, u32[]{:S(2)}) copy-start(bf16[128,128]{1,0:T(8,128)(2,1)} %param.17) | copy-start | bytes 98308
  87.4 0.8 copy-start.5
  87.4 0.8 copy-start.7

commit v2 on v0

v2 whole, which is shorter than its diff:
```python
import functools

import jax
import jax.numpy as jnp
from jax import lax
from jax.experimental import pallas as pl
from jax.experimental.pallas import tpu as pltpu
from jax.sharding import PartitionSpec as P

MESH = pl.DeviceIdType.MESH
BF16, F32 = jnp.bfloat16, jnp.float32
EPS = 1e-05


def dot_nt(a, b):
    return lax.dot_general(a, b, (((1,), (1,)), ((), ())), preferred_element_type=F32)


def iota(shape, axis):
    return lax.broadcasted_iota(jnp.int32, shape, axis)


def sigmoid(x):
    return jax.nn.sigmoid(x)


def kernel(
    north,
    east,
    rows,
    cols,
    x_ref,
    in_gain_ref,
    lw_ref,
    rw_ref,
    lg_ref,
    rg_ref,
    mid_gain_ref,
    ow_ref,
    og_ref,
    out_ref,
    ready_ref,
    gate_ref,
    send1,
    recv1,
    left_ref,
    right_ref,
    send2,
    recv2,
    send_sem1,
    recv_sem1,
    send_sem2,
    recv_sem2,
):
    width = x_ref.shape[1]
    group = north * east
    half = rows // 2
    lines = half * cols
    n = lax.axis_index("north")
    e = lax.axis_index("east")
    me = e * north + n

    def device(c, k):
        return lax.rem(e + c, east), lax.rem(n + k, north)

    def each_peer(do):
        for c in range(east):

            def body(k, carry, c=c):
                do(*device(c, k))
                return carry

            lax.fori_loop(1 if c == 0 else 0, north, body, 0)

    barrier = pltpu.get_barrier_semaphore()
    each_peer(
        lambda pe, pn: pl.semaphore_signal(
            barrier, inc=1, device_id={"north": pn, "east": pe}, device_id_type=MESH
        )
    )

    x = x_ref[...].astype(F32)
    centred = x - jnp.mean(x, axis=-1, keepdims=True)
    ready = (
        centred * lax.rsqrt(jnp.mean(centred * centred, axis=-1, keepdims=True) + EPS)
        * in_gain_ref[...]
    ).astype(BF16)
    ready_ref[...] = ready
    both = jnp.concatenate([ready_ref[:lines, :], ready_ref[lines:, :]], axis=1)

    def send_all(src, dst, send_sem, recv_sem):
        dst[me] = src[me]
        each_peer(
            lambda pe, pn: pltpu.make_async_remote_copy(
                src_ref=src.at[pe * north + pn],
                dst_ref=dst.at[me],
                send_sem=send_sem,
                recv_sem=recv_sem,
                device_id={"north": pn, "east": pe},
                device_id_type=MESH,
            ).start()
        )

    def all_of(src, dst, send_sem, recv_sem):
        return pltpu.make_async_remote_copy(
            src_ref=src.at[pl.ds(0, group - 1)],
            dst_ref=dst.at[pl.ds(0, group - 1)],
            send_sem=send_sem,
            recv_sem=recv_sem,
            device_id={"north": n, "east": e},
            device_id_type=MESH,
        )

    r = iota((4 * group, width), 0)
    d = iota((4 * group, width), 1)
    parity = (r & 1) == 0

    def spread(weights, ch):
        picked = 0.0
        for f, w in enumerate(weights):
            pick = (((r >> 1) & 1) == f) & (d == (r >> 2) + ch * group)
            picked = picked + dot_nt(jnp.where(pick, 1.0, 0.0).astype(BF16), w[...])
        return jnp.concatenate(
            [jnp.where(parity, picked, 0.0), jnp.where(parity, 0.0, picked)], axis=1
        ).astype(BF16)

    for ch in range(2):
        value = dot_nt(spread((lw_ref, rw_ref), ch), both)
        gate = dot_nt(spread((lg_ref, rg_ref), ch), both)
        value = (value * sigmoid(gate)).reshape(group, 4, lines)
        send1[ch] = value.astype(BF16)
        if ch == 0:
            pl.semaphore_wait(barrier, group - 1)
        send_all(send1.at[ch], recv1.at[ch], send_sem1.at[ch], recv_sem1.at[ch])

    gate_ref[...] = sigmoid(
        jnp.dot(ready_ref[...], og_ref[...], preferred_element_type=F32)
    )
    left_ref[...] = jnp.zeros_like(left_ref)
    right_ref[...] = jnp.zeros_like(right_ref)

    per = north // east * 2
    for ch in range(2):
        all_of(send1.at[ch], recv1.at[ch], send_sem1.at[ch], recv_sem1.at[ch]).wait_recv()
        for s in range(east):
            lines_l = recv1[ch, north * s : north * (s + 1), 0:2, :].reshape(2 * north, lines)
            lines_r = recv1[ch, north * s : north * (s + 1), 2:4, :].reshape(2 * north, lines)
            for i in range(half):
                left_ref[2 * north * i : 2 * north * (i + 1), 128 * s : 128 * s + cols] = (
                    lines_l[:, cols * i : cols * (i + 1)]
                )
                piece = lines_r[:, cols * i : cols * (i + 1)]
                for t in range(east):
                    right_ref[128 * t + per * i : 128 * t + per * (i + 1), 128 * s : 128 * s + cols] = (
                        piece[per * t : per * (t + 1)]
                    )
        mixed = dot_nt(left_ref[...], right_ref[...]) * (cols * east) ** (-0.5)
        for t in range(east):
            strip = jnp.concatenate(
                [
                    mixed[2 * north * i : 2 * north * (i + 1), 128 * t : 128 * t + cols]
                    for i in range(half)
                ],
                axis=1,
            )
            send2[ch, north * t : north * (t + 1)] = strip.reshape(north, 2, lines).astype(BF16)
        send_all(send2.at[ch], recv2.at[ch], send_sem2.at[ch], recv_sem2.at[ch])

    mid_gain = jnp.broadcast_to(mid_gain_ref[...], (width, width)).T
    mid_gain = jnp.broadcast_to(mid_gain[:, None, :], (width, 2, width)).reshape(2 * width, width)
    mid_gain = jnp.concatenate([mid_gain] * 3, axis=1)
    weight = ow_ref[...].astype(F32)
    weight = jnp.broadcast_to(weight[:, None, :], (width, 2, width)).reshape(2 * width, width)
    first = (iota((2 * width, width), 0) & 1) == 0
    weight = jnp.concatenate(
        [jnp.where(first, weight, 0.0), jnp.where(first, 0.0, weight)], axis=1
    ).astype(BF16)
    tile = 4 * cols
    lane = iota((tile, tile), 1)
    block = jnp.where(lane >= 2 * cols, 2, 0)
    block = block + jnp.where(lane - block * cols >= cols, 1, 0)
    rest = lane - block * cols
    target = block * cols + ((rest & (per - 1)) >> 1) * rows + (rest & 1) * half + (rest >> 3)
    order = jnp.where(iota((tile, tile), 0) == target, 1.0, 0.0).astype(BF16)

    for ch in range(2):
        all_of(send2.at[ch], recv2.at[ch], send_sem2.at[ch], recv_sem2.at[ch]).wait_recv()

    def fold(total):
        total = jnp.sum(total.reshape(2 * width // 8, 8, tile), axis=0)
        total = total + pltpu.roll(total, 4, 0)
        total = total + pltpu.roll(total, 2, 0)
        return (total * (1.0 / width))[None]

    for g in range(lines // tile):
        lanes = slice(g * tile, (g + 1) * tile)
        mixed = recv2[:, :, :, lanes].reshape(2 * width, tile).astype(F32)
        centred = mixed.reshape(2 * width // 8, 8, tile) - fold(mixed)
        scale = lax.rsqrt(fold((centred * centred).reshape(2 * width, tile)) + EPS)
        scaled = ((centred * scale).reshape(2 * width, tile) * mid_gain).astype(BF16)
        turned = dot_nt(order, scaled).astype(BF16)
        result = jnp.dot(turned, weight, preferred_element_type=F32)
        for h in range(2):
            at = slice(h * lines + g * tile, h * lines + (g + 1) * tile)
            out_ref[at, :] = (
                result[:, h * width : (h + 1) * width] * gate_ref[at, :]
            ).astype(BF16)

    for ch in range(2):
        for src, dst, a, b in (
            (send1, recv1, send_sem1, recv_sem1),
            (send2, recv2, send_sem2, recv_sem2),
        ):
            all_of(src.at[ch], dst.at[ch], a.at[ch], b.at[ch]).wait_send()


def local(
    north,
    east,
    pair_state,
    in_gain,
    left_weight,
    right_weight,
    left_gate,
    right_gate,
    mid_gain,
    out_weight,
    out_gate,
):
    rows, cols, width = pair_state.shape
    lines = rows // 2 * cols
    group = north * east
    vmem = pl.BlockSpec(memory_space=pltpu.VMEM)
    out = pl.pallas_call(
        functools.partial(kernel, north, east, rows, cols),
        out_shape=jax.ShapeDtypeStruct((rows * cols, width), BF16),
        in_specs=[vmem] * 9,
        out_specs=vmem,
        scratch_shapes=[
            pltpu.VMEM((rows * cols, width), BF16),
            pltpu.VMEM((rows * cols, width), F32),
            pltpu.VMEM((2, group, 4, lines), BF16),
            pltpu.VMEM((2, group, 4, lines), BF16),
            pltpu.VMEM((rows * north, 128 * east), BF16),
            pltpu.VMEM((128 * east, 128 * east), BF16),
            pltpu.VMEM((2, group, 2, lines), BF16),
            pltpu.VMEM((2, group, 2, lines), BF16),
            pltpu.SemaphoreType.DMA((2,)),
            pltpu.SemaphoreType.DMA((2,)),
            pltpu.SemaphoreType.DMA((2,)),
            pltpu.SemaphoreType.DMA((2,)),
        ],
        compiler_params=pltpu.CompilerParams(
            collective_id=0, has_side_effects=True, vmem_limit_bytes=48 * 1024 * 1024
        ),
    )(
        pair_state.reshape(rows * cols, width),
        in_gain.reshape(1, width),
        left_weight,
        right_weight,
        left_gate,
        right_gate,
        mid_gain.reshape(1, width),
        out_weight,
        out_gate,
    )
    return out.reshape(rows, cols, width)


def solution(mesh):
    north, east = mesh.shape["north"], mesh.shape["east"]
    return jax.shard_map(
        functools.partial(local, north, east),
        mesh=mesh,
        in_specs=(
            P(("trial", "north"), "east", None),
            P(),
            P("trial", None),
            P("trial", None),
            P("trial", None),
            P("trial", None),
            P(),
            P("trial", None),
            P("trial", None),
        ),
        out_specs=P(("trial", "north"), "east", None),
        check_vma=False,
    )
```

time: 277 us -> 62.6 us (0.23)
  waiting for transfers between devices: 168 us -> 0 us
  blocking collectives: 56.4 us -> 0 us
  Pallas kernels: 0 us -> 55 us
  between operations: 13.6 us -> 0.02 us
  matrix products: 11.1 us -> 0 us
  local copies, waits for them, and re-layouts: 16.7 us -> 7.09 us
  other arithmetic: 4.88 us -> 0 us
  starting transfers between devices: 3.61 us -> 0 us
    all_gather x1 -> x0, waiting for transfers between devices: 153 us -> none  [local(): lax.all_gather(right_lines, 'north', axis=0, tiled=True)]
    all_to_all x2 -> x0, blocking collectives: 56.4 us -> none  [the longest x1 30.6 us: local(): lax.all_to_all(left, 'east', split_axis=2, concat_axis=1, tiled=True)]
    pallas_call x0 -> x1, Pallas kernels: none -> 55 us  [local(): pl.pallas_call(functools.partial(kernel, north, east, rows, cols), out_sh...]
    all_to_all x1 -> x0, waiting for transfers between devices: 14.9 us -> none  [local(): lax.all_to_all(strip, 'east', split_axis=1, concat_axis=2, tiled=True)]
    dot_general x7 -> x0, matrix products: 11.1 us -> none  [the longest x1 7.89 us: local(): jnp.einsum('ikd,jkd->ijd', left_lines, lax.all_gather(right_lines, 'north...]
    convert_element_type x4 -> x0, local copies, waits for them, and re-layouts: 6.59 us -> none  [the longest x1 3.03 us: local(): strip = (strip * count ** (-0.5)).astype(jnp.bfloat16)]
    reduce_sum x4 -> x0, other arithmetic: 3.71 us -> none  [the longest x2 2.11 us: norm_channels(): jnp.mean(centred * centred, axis=-1, keepdims=True) + 1e-05]
    all_to_all x1 -> x0, starting transfers between devices: 3.61 us -> none  [local(): lax.all_to_all(strip, 'east', split_axis=1, concat_axis=2, tiled=True)]
  transfers between devices with their start and end apart: 2 -> 0, of which waited for: 2 -> 0; matrix products, arithmetic and copies ran while one was open for 1% -> 0% of each run, Pallas kernels for 0% -> 0%
where the time goes in v2:
time: 62.6 us; the launch traced here: 62.1 us
  Pallas kernels  55 us (88%)
  local copies, waits for them, and re-layouts  7.09 us (11%)
    pallas_call x1, Pallas kernels, local(): pl.pallas_call(functools.partial(kernel, north, east, rows, cols), out_sh...  55 us
    unnamed x19, local copies, waits for them, and re-layouts  7.09 us

profile of v2, /device:TPU:8, one launch (start us, length us, event | category | flops | bytes accessed | tf_op | source)
XLA Modules:
  0.0 62.1 jit_solution(12822048801280982396)
XLA Ops:
  0.0 0.0 copy-start.7
  0.0 0.0 copy-start.8
  0.0 0.7 %copy-done.7 = f32[128]{0:T(128)S(1)} copy-done((f32[128]{0:T(128)S(1)}, f32[128]{0:T(128)}, u32[]{:S(2)}) %copy-start.7) | copy-done | bytes 536
  0.7 0.0 copy-done.8
  0.7 0.0 copy-start
  0.7 1.1 %copy-done = bf16[24,96,128]{2,1,0:T(8,128)(2,1)S(1)} copy-done((bf16[24,96,128]{2,1,0:T(8,128)(2,1)S(1)}, bf16[24,96,128]{2,1,0:T(8,128)(2,1)}, u32[]{:S(2)}) %copy-start) | copy-done | bytes 589848
  1.7 0.0 copy-start.1
  1.7 0.8 %copy-done.1 = bf16[128,128]{1,0:T(8,128)(2,1)S(1)} copy-done((bf16[128,128]{1,0:T(8,128)(2,1)S(1)}, bf16[128,128]{1,0:T(8,128)(2,1)}, u32[]{:S(2)}) %copy-start.1) | copy-done | bytes 32792
  2.5 0.0 copy-start.2
  2.5 0.8 %copy-done.2 = bf16[128,128]{1,0:T(8,128)(2,1)S(1)} copy-done((bf16[128,128]{1,0:T(8,128)(2,1)S(1)}, bf16[128,128]{1,0:T(8,128)(2,1)}, u32[]{:S(2)}) %copy-start.2) | copy-done | bytes 32792
  3.3 0.0 copy-start.3
  3.3 0.8 %copy-done.3 = bf16[128,128]{1,0:T(8,128)(2,1)S(1)} copy-done((bf16[128,128]{1,0:T(8,128)(2,1)S(1)}, bf16[128,128]{1,0:T(8,128)(2,1)}, u32[]{:S(2)}) %copy-start.3) | copy-done | bytes 32792
  4.0 0.0 copy-start.4
  4.0 0.8 %copy-done.4 = bf16[128,128]{1,0:T(8,128)(2,1)S(1)} copy-done((bf16[128,128]{1,0:T(8,128)(2,1)S(1)}, bf16[128,128]{1,0:T(8,128)(2,1)}, u32[]{:S(2)}) %copy-start.4) | copy-done | bytes 32792
  4.8 0.0 copy-start.5
  4.8 0.8 %copy-done.5 = bf16[128,128]{1,0:T(8,128)(2,1)S(1)} copy-done((bf16[128,128]{1,0:T(8,128)(2,1)S(1)}, bf16[128,128]{1,0:T(8,128)(2,1)}, u32[]{:S(2)}) %copy-start.5) | copy-done | bytes 32792
  5.5 0.0 copy-start.6
  5.5 0.8 %copy-done.6 = bf16[128,128]{1,0:T(8,128)(2,1)S(1)} copy-done((bf16[128,128]{1,0:T(8,128)(2,1)S(1)}, bf16[128,128]{1,0:T(8,128)(2,1)}, u32[]{:S(2)}) %copy-start.6) | copy-done | bytes 32792
  6.3 55.0 %shard_map.91 = bf16[2304,128]{1,0:T(8,128)(2,1)S(1)} custom-call(bf16[2304,128]{1,0:T(8,128)(2,1)S(1)} %bitcast.5, f32[1,128]{1,0:T(1,128)S(1)} %bitcast.6, bf16[128,128]{1,0:T(8,128)(2,1)S(1)} %copy-done.1, bf16[128,128]{1,0:T(8,128)(2,1)S(1)} %copy-done.2, bf16[128,128]{1,0:T(8,128)(2,1)S(1)} %copy-done.3, bf16[128,128]{1,0:T(8,128)(2,1)S(1)} %copy-done.4, ...), custom_call_target="tpu_custom_call" | custom-call | tf_op jit(solution)/shard_map/pallas_call | solution.py:234
  61.3 0.8 %copy.11 = bf16[24,96,128]{2,1,0:T(8,128)(2,1)} copy(bf16[24,96,128]{2,1,0:T(8,128)(2,1)S(1)} %bitcast.4) | data formatting | bytes 1179648
Async XLA Ops:
  0.0 0.7 %copy-start.7 = (f32[128]{0:T(128)S(1)}, f32[128]{0:T(128)}, u32[]{:S(2)}) copy-start(f32[128]{0:T(128)} %param.10) | copy-start | bytes 1540
  0.0 0.7 %copy-start.8 = (f32[128]{0:T(128)S(1)}, f32[128]{0:T(128)}, u32[]{:S(2)}) copy-start(f32[128]{0:T(128)} %param.15) | copy-start | bytes 1540
  0.7 1.1 %copy-start = (bf16[24,96,128]{2,1,0:T(8,128)(2,1)S(1)}, bf16[24,96,128]{2,1,0:T(8,128)(2,1)}, u32[]{:S(2)}) copy-start(bf16[24,96,128]{2,1,0:T(8,128)(2,1)} %param.9) | copy-start | bytes 1769476
  1.7 0.8 %copy-start.1 = (bf16[128,128]{1,0:T(8,128)(2,1)S(1)}, bf16[128,128]{1,0:T(8,128)(2,1)}, u32[]{:S(2)}) copy-start(bf16[128,128]{1,0:T(8,128)(2,1)} %lw_ref.1) | copy-start | bytes 98308
  2.5 0.8 %copy-start.2 = (bf16[128,128]{1,0:T(8,128)(2,1)S(1)}, bf16[128,128]{1,0:T(8,128)(2,1)}, u32[]{:S(2)}) copy-start(bf16[128,128]{1,0:T(8,128)(2,1)} %rw_ref.1) | copy-start | bytes 98308
  3.3 0.8 %copy-start.3 = (bf16[128,128]{1,0:T(8,128)(2,1)S(1)}, bf16[128,128]{1,0:T(8,128)(2,1)}, u32[]{:S(2)}) copy-start(bf16[128,128]{1,0:T(8,128)(2,1)} %lg_ref.1) | copy-start | bytes 98308
  4.0 0.8 %copy-start.4 = (bf16[128,128]{1,0:T(8,128)(2,1)S(1)}, bf16[128,128]{1,0:T(8,128)(2,1)}, u32[]{:S(2)}) copy-start(bf16[128,128]{1,0:T(8,128)(2,1)} %rg_ref.1) | copy-start | bytes 98308
  4.8 0.8 %copy-start.5 = (bf16[128,128]{1,0:T(8,128)(2,1)S(1)}, bf16[128,128]{1,0:T(8,128)(2,1)}, u32[]{:S(2)}) copy-start(bf16[128,128]{1,0:T(8,128)(2,1)} %ow_ref.1) | copy-start | bytes 98308
  5.5 0.8 %copy-start.6 = (bf16[128,128]{1,0:T(8,128)(2,1)S(1)}, bf16[128,128]{1,0:T(8,128)(2,1)}, u32[]{:S(2)}) copy-start(bf16[128,128]{1,0:T(8,128)(2,1)} %og_ref.1) | copy-start | bytes 98308

commit v3 on v2

--- a/solution.py
+++ b/solution.py
@@ -29,6 +29,16 @@
     east,
     rows,
     cols,
+    x_hbm,
+    in_gain_hbm,
+    lw_hbm,
+    rw_hbm,
+    lg_hbm,
+    rg_hbm,
+    mid_gain_hbm,
+    ow_hbm,
+    og_hbm,
+    out_ref,
     x_ref,
     in_gain_ref,
     lw_ref,
@@ -38,7 +48,7 @@
     mid_gain_ref,
     ow_ref,
     og_ref,
-    out_ref,
+    load_sem,
     ready_ref,
     gate_ref,
     send1,
@@ -52,6 +62,24 @@
     send_sem2,
     recv_sem2,
 ):
+    loads = [
+        pltpu.make_async_copy(src, dst, load_sem.at[i])
+        for i, (src, dst) in enumerate(
+            (
+                (x_hbm, x_ref),
+                (in_gain_hbm, in_gain_ref),
+                (lw_hbm, lw_ref),
+                (rw_hbm, rw_ref),
+                (lg_hbm, lg_ref),
+                (rg_hbm, rg_ref),
+                (mid_gain_hbm, mid_gain_ref),
+                (ow_hbm, ow_ref),
+                (og_hbm, og_ref),
+            )
+        )
+    ]
+    for load in loads:
+        load.start()
     width = x_ref.shape[1]
     group = north * east
     half = rows // 2
@@ -78,6 +106,9 @@
             barrier, inc=1, device_id={"north": pn, "east": pe}, device_id_type=MESH
         )
     )
+
+    for load in loads:
+        load.wait()
 
     x = x_ref[...].astype(F32)
     centred = x - jnp.mean(x, axis=-1, keepdims=True)
@@ -234,9 +265,19 @@
     out = pl.pallas_call(
         functools.partial(kernel, north, east, rows, cols),
         out_shape=jax.ShapeDtypeStruct((rows * cols, width), BF16),
-        in_specs=[vmem] * 9,
+        in_specs=[pl.BlockSpec(memory_space=pltpu.HBM)] * 9,
         out_specs=vmem,
         scratch_shapes=[
+            pltpu.VMEM((rows * cols, width), BF16),
+            pltpu.VMEM((1, width), F32),
+            pltpu.VMEM((width, width), BF16),
+            pltpu.VMEM((width, width), BF16),
+            pltpu.VMEM((width, width), BF16),
+            pltpu.VMEM((width, width), BF16),
+            pltpu.VMEM((1, width), F32),
+            pltpu.VMEM((width, width), BF16),
+            pltpu.VMEM((width, width), BF16),
+            pltpu.SemaphoreType.DMA((9,)),
             pltpu.VMEM((rows * cols, width), BF16),
             pltpu.VMEM((rows * cols, width), F32),
             pltpu.VMEM((2, group, 4, lines), BF16),

time: 62.6 us -> 63.6 us (1.016)
  Pallas kernels: 55 us -> 56 us
    pallas_call x1, Pallas kernels: 55 us -> 56 us  [local(): pl.pallas_call(functools.partial(kernel, north, east, rows, cols), out_sh...]
where the time goes in v3:
time: 63.6 us; the launch traced here: 63.1 us
  Pallas kernels  56 us (88%)
  local copies, waits for them, and re-layouts  7.09 us (11%)
    pallas_call x1, Pallas kernels, local(): pl.pallas_call(functools.partial(kernel, north, east, rows, cols), out_sh...  56 us
    unnamed x19, local copies, waits for them, and re-layouts  7.09 us

profile of v3, /device:TPU:8, one launch (start us, length us, event | category | flops | bytes accessed | tf_op | source)
XLA Modules:
  0.0 63.1 jit_solution(5461940749646122351)
XLA Ops:
  0.0 0.0 copy-start.7
  0.0 0.0 copy-start.8
  0.0 0.7 %copy-done.7 = f32[128]{0:T(128)S(1)} copy-done((f32[128]{0:T(128)S(1)}, f32[128]{0:T(128)}, u32[]{:S(2)}) %copy-start.7) | copy-done | bytes 536
  0.7 0.0 copy-done.8
  0.7 0.0 copy-start
  0.7 1.1 %copy-done = bf16[24,96,128]{2,1,0:T(8,128)(2,1)S(1)} copy-done((bf16[24,96,128]{2,1,0:T(8,128)(2,1)S(1)}, bf16[24,96,128]{2,1,0:T(8,128)(2,1)}, u32[]{:S(2)}) %copy-start) | copy-done | bytes 589848
  1.7 0.0 copy-start.1
  1.7 0.8 %copy-done.1 = bf16[128,128]{1,0:T(8,128)(2,1)S(1)} copy-done((bf16[128,128]{1,0:T(8,128)(2,1)S(1)}, bf16[128,128]{1,0:T(8,128)(2,1)}, u32[]{:S(2)}) %copy-start.1) | copy-done | bytes 32792
  2.5 0.0 copy-start.2
  2.5 0.8 %copy-done.2 = bf16[128,128]{1,0:T(8,128)(2,1)S(1)} copy-done((bf16[128,128]{1,0:T(8,128)(2,1)S(1)}, bf16[128,128]{1,0:T(8,128)(2,1)}, u32[]{:S(2)}) %copy-start.2) | copy-done | bytes 32792
  3.3 0.0 copy-start.3
  3.3 0.8 %copy-done.3 = bf16[128,128]{1,0:T(8,128)(2,1)S(1)} copy-done((bf16[128,128]{1,0:T(8,128)(2,1)S(1)}, bf16[128,128]{1,0:T(8,128)(2,1)}, u32[]{:S(2)}) %copy-start.3) | copy-done | bytes 32792
  4.0 0.0 copy-start.4
  4.0 0.8 %copy-done.4 = bf16[128,128]{1,0:T(8,128)(2,1)S(1)} copy-done((bf16[128,128]{1,0:T(8,128)(2,1)S(1)}, bf16[128,128]{1,0:T(8,128)(2,1)}, u32[]{:S(2)}) %copy-start.4) | copy-done | bytes 32792
  4.8 0.0 copy-start.5
  4.8 0.8 %copy-done.5 = bf16[128,128]{1,0:T(8,128)(2,1)S(1)} copy-done((bf16[128,128]{1,0:T(8,128)(2,1)S(1)}, bf16[128,128]{1,0:T(8,128)(2,1)}, u32[]{:S(2)}) %copy-start.5) | copy-done | bytes 32792
  5.5 0.0 copy-start.6
  5.5 0.8 %copy-done.6 = bf16[128,128]{1,0:T(8,128)(2,1)S(1)} copy-done((bf16[128,128]{1,0:T(8,128)(2,1)S(1)}, bf16[128,128]{1,0:T(8,128)(2,1)}, u32[]{:S(2)}) %copy-start.6) | copy-done | bytes 32792
  6.3 56.0 %shard_map.91 = bf16[2304,128]{1,0:T(8,128)(2,1)S(1)} custom-call(bf16[2304,128]{1,0:T(8,128)(2,1)S(1)} %bitcast.5, f32[1,128]{1,0:T(1,128)S(1)} %bitcast.6, bf16[128,128]{1,0:T(8,128)(2,1)S(1)} %copy-done.1, bf16[128,128]{1,0:T(8,128)(2,1)S(1)} %copy-done.2, bf16[128,128]{1,0:T(8,128)(2,1)S(1)} %copy-done.3, bf16[128,128]{1,0:T(8,128)(2,1)S(1)} %copy-done.4, ...), custom_call_target="tpu_custom_call" | custom-call | tf_op jit(solution)/shard_map/pallas_call | solution.py:265
  62.3 0.8 %copy.11 = bf16[24,96,128]{2,1,0:T(8,128)(2,1)} copy(bf16[24,96,128]{2,1,0:T(8,128)(2,1)S(1)} %bitcast.4) | data formatting | bytes 1179648
Async XLA Ops:
  0.0 0.7 %copy-start.7 = (f32[128]{0:T(128)S(1)}, f32[128]{0:T(128)}, u32[]{:S(2)}) copy-start(f32[128]{0:T(128)} %param.10) | copy-start | bytes 1540
  0.0 0.7 %copy-start.8 = (f32[128]{0:T(128)S(1)}, f32[128]{0:T(128)}, u32[]{:S(2)}) copy-start(f32[128]{0:T(128)} %param.15) | copy-start | bytes 1540
  0.7 1.1 %copy-start = (bf16[24,96,128]{2,1,0:T(8,128)(2,1)S(1)}, bf16[24,96,128]{2,1,0:T(8,128)(2,1)}, u32[]{:S(2)}) copy-start(bf16[24,96,128]{2,1,0:T(8,128)(2,1)} %param.9) | copy-start | bytes 1769476
  1.7 0.8 %copy-start.1 = (bf16[128,128]{1,0:T(8,128)(2,1)S(1)}, bf16[128,128]{1,0:T(8,128)(2,1)}, u32[]{:S(2)}) copy-start(bf16[128,128]{1,0:T(8,128)(2,1)} %lw_hbm.1) | copy-start | bytes 98308
  2.5 0.8 %copy-start.2 = (bf16[128,128]{1,0:T(8,128)(2,1)S(1)}, bf16[128,128]{1,0:T(8,128)(2,1)}, u32[]{:S(2)}) copy-start(bf16[128,128]{1,0:T(8,128)(2,1)} %rw_hbm.1) | copy-start | bytes 98308
  3.3 0.8 %copy-start.3 = (bf16[128,128]{1,0:T(8,128)(2,1)S(1)}, bf16[128,128]{1,0:T(8,128)(2,1)}, u32[]{:S(2)}) copy-start(bf16[128,128]{1,0:T(8,128)(2,1)} %lg_hbm.1) | copy-start | bytes 98308
  4.0 0.8 %copy-start.4 = (bf16[128,128]{1,0:T(8,128)(2,1)S(1)}, bf16[128,128]{1,0:T(8,128)(2,1)}, u32[]{:S(2)}) copy-start(bf16[128,128]{1,0:T(8,128)(2,1)} %rg_hbm.1) | copy-start | bytes 98308
  4.8 0.8 %copy-start.5 = (bf16[128,128]{1,0:T(8,128)(2,1)S(1)}, bf16[128,128]{1,0:T(8,128)(2,1)}, u32[]{:S(2)}) copy-start(bf16[128,128]{1,0:T(8,128)(2,1)} %ow_hbm.1) | copy-start | bytes 98308
  5.5 0.8 %copy-start.6 = (bf16[128,128]{1,0:T(8,128)(2,1)S(1)}, bf16[128,128]{1,0:T(8,128)(2,1)}, u32[]{:S(2)}) copy-start(bf16[128,128]{1,0:T(8,128)(2,1)} %og_hbm.1) | copy-start | bytes 98308

commit v4 on v3

--- a/solution.py
+++ b/solution.py
@@ -292,7 +292,7 @@
             pltpu.SemaphoreType.DMA((2,)),
         ],
         compiler_params=pltpu.CompilerParams(
-            collective_id=0, has_side_effects=True, vmem_limit_bytes=48 * 1024 * 1024
+            collective_id=0, has_side_effects=True, vmem_limit_bytes=67_043_328
         ),
     )(
         pair_state.reshape(rows * cols, width),

time: 63.6 us -> 58.5 us (0.920)
  local copies, waits for them, and re-layouts: 7.09 us -> 1.92 us
    unnamed x19 -> x1, local copies, waits for them, and re-layouts: 7.09 us -> 1.92 us
where the time goes in v4:
time: 58.5 us; the launch traced here: 58.4 us
  Pallas kernels  56.4 us (96%)
  local copies, waits for them, and re-layouts  1.92 us (3%)
    pallas_call x1, Pallas kernels, local(): pl.pallas_call(functools.partial(kernel, north, east, rows, cols), out_sh...  56.4 us
    unnamed x1, local copies, waits for them, and re-layouts  1.92 us

profile of v4, /device:TPU:8, one launch (start us, length us, event | category | flops | bytes accessed | tf_op | source)
XLA Modules:
  0.0 58.4 jit_solution(4958026973734409018)
XLA Ops:
  0.0 56.4 %shard_map.91 = bf16[2304,128]{1,0:T(8,128)(2,1)} custom-call(bf16[2304,128]{1,0:T(8,128)(2,1)} %bitcast.5, f32[1,128]{1,0:T(1,128)} %bitcast.6, bf16[128,128]{1,0:T(8,128)(2,1)} %lw_hbm.1, bf16[128,128]{1,0:T(8,128)(2,1)} %rw_hbm.1, bf16[128,128]{1,0:T(8,128)(2,1)} %lg_hbm.1, bf16[128,128]{1,0:T(8,128)(2,1)} %rg_hbm.1, f32[1,128]{1,0:T(1,128)} %bitcast.7, ...), custom_call_target="tpu_custom_call" | custom-call | tf_op jit(solution)/shard_map/pallas_call | solution.py:265
  56.4 1.9 %copy.11 = bf16[24,96,128]{2,1,0:T(8,128)(2,1)} copy(bf16[24,96,128]{2,1,0:T(8,128)(2,1)} %bitcast.4) | data formatting | bytes 1179648

commit v5 on v3

--- a/solution.py
+++ b/solution.py
@@ -264,7 +264,7 @@
     vmem = pl.BlockSpec(memory_space=pltpu.VMEM)
     out = pl.pallas_call(
         functools.partial(kernel, north, east, rows, cols),
-        out_shape=jax.ShapeDtypeStruct((rows * cols, width), BF16),
+        out_shape=pltpu.VMEM((rows * cols, width), BF16),
         in_specs=[pl.BlockSpec(memory_space=pltpu.HBM)] * 9,
         out_specs=vmem,
         scratch_shapes=[
@@ -295,15 +295,20 @@
             collective_id=0, has_side_effects=True, vmem_limit_bytes=48 * 1024 * 1024
         ),
     )(
-        pair_state.reshape(rows * cols, width),
-        in_gain.reshape(1, width),
-        left_weight,
-        right_weight,
-        left_gate,
-        right_gate,
-        mid_gain.reshape(1, width),
-        out_weight,
-        out_gate,
+        *(
+            pltpu.with_memory_space_constraint(a, pltpu.HBM)
+            for a in (
+                pair_state.reshape(rows * cols, width),
+                in_gain.reshape(1, width),
+                left_weight,
+                right_weight,
+                left_gate,
+                right_gate,
+                mid_gain.reshape(1, width),
+                out_weight,
+                out_gate,
+            )
+        )
     )
     return out.reshape(rows, cols, width)
 

time: 63.6 us -> 56.5 us (0.89)
  local copies, waits for them, and re-layouts: 7.09 us -> 0.82 us
    unnamed x19 -> x1, local copies, waits for them, and re-layouts: 7.09 us -> 0.82 us
where the time goes in v5:
time: 56.5 us; the launch traced here: 56.4 us
  Pallas kernels  55.6 us (98%)
  local copies, waits for them, and re-layouts  0.82 us (1%)
    pallas_call x1, Pallas kernels, local(): pl.pallas_call(functools.partial(kernel, north, east, rows, cols), out_sh...  55.6 us

profile of v5, /device:TPU:8, one launch (start us, length us, event | category | flops | bytes accessed | tf_op | source)
XLA Modules:
  0.0 56.4 jit_solution(10194785756802895267)
XLA Ops:
  0.0 55.6 %shard_map.91 = bf16[2304,128]{1,0:T(8,128)(2,1)S(1)} custom-call(bf16[2304,128]{1,0:T(8,128)(2,1)} %bitcast.5, f32[1,128]{1,0:T(1,128)} %bitcast.6, bf16[128,128]{1,0:T(8,128)(2,1)} %lw_hbm.1, bf16[128,128]{1,0:T(8,128)(2,1)} %rw_hbm.1, bf16[128,128]{1,0:T(8,128)(2,1)} %lg_hbm.1, bf16[128,128]{1,0:T(8,128)(2,1)} %rg_hbm.1, f32[1,128]{1,0:T(1,128)} %bitcast.7, ...), custom_call_target="tpu_custom_call" | custom-call | tf_op jit(solution)/shard_map/pallas_call | solution.py:265
  55.6 0.8 %copy.11 = bf16[24,96,128]{2,1,0:T(8,128)(2,1)} copy(bf16[24,96,128]{2,1,0:T(8,128)(2,1)S(1)} %bitcast.4) | data formatting | bytes 1179648

commit v6 on v5

--- a/solution.py
+++ b/solution.py
@@ -9,6 +9,7 @@
 
 MESH = pl.DeviceIdType.MESH
 BF16, F32 = jnp.bfloat16, jnp.float32
+Y, X = 4, 2
 EPS = 1e-05
 
 
@@ -61,6 +62,8 @@
     recv_sem1,
     send_sem2,
     recv_sem2,
+    known,
+    spread_ref,
 ):
     loads = [
         pltpu.make_async_copy(src, dst, load_sem.at[i])
@@ -88,28 +91,97 @@
     e = lax.axis_index("east")
     me = e * north + n
 
-    def device(c, k):
-        return lax.rem(e + c, east), lax.rem(n + k, north)
-
-    def each_peer(do):
-        for c in range(east):
-
-            def body(k, carry, c=c):
-                do(*device(c, k))
-                return carry
-
-            lax.fori_loop(1 if c == 0 else 0, north, body, 0)
+    at_z, at_y, at_x = n // (Y * X) * east + e, lax.rem(n // X, Y), lax.rem(n, X)
+    depth = group // (Y * X)
+    everyone = [(a, b, c) for a in range(depth) for b in range(Y) for c in range(X)][1:]
+    everyone.sort(key=lambda o: -min(o[0], depth - o[0]) - min(o[1], Y - o[1]) - 2 * o[2])
+    columns = [o for o in everyone if o[0] == 0]
+    near = [o for o in everyone if o in columns or o[1:] == (0, 0)]
+    rest = [o for o in everyone if o not in near]
+
+    def each_peer(offsets, do):
+        for dz, dy, dx in offsets:
+            pz = lax.rem(at_z + dz, depth)
+            north_of = (pz // east * Y + lax.rem(at_y + dy, Y)) * X + lax.rem(at_x + dx, X)
+            east_of = lax.rem(pz, east)
+            do(east_of * north + north_of, {"north": north_of, "east": east_of})
+
+    def signal(semaphore, offsets):
+        each_peer(
+            offsets,
+            lambda q, device: pl.semaphore_signal(
+                semaphore, inc=1, device_id=device, device_id_type=MESH
+            ),
+        )
 
     barrier = pltpu.get_barrier_semaphore()
-    each_peer(
-        lambda pe, pn: pl.semaphore_signal(
-            barrier, inc=1, device_id={"north": pn, "east": pe}, device_id_type=MESH
-        )
-    )
-
-    for load in loads:
+    signal(barrier, near)
+
+    def send(src, dst, send_sem, recv_sem, offsets):
+        each_peer(
+            offsets,
+            lambda q, device: pltpu.make_async_remote_copy(
+                src_ref=src(q),
+                dst_ref=dst(me),
+                send_sem=send_sem,
+                recv_sem=recv_sem,
+                device_id=device,
+                device_id_type=MESH,
+            ).start(),
+        )
+
+    def all_of(src, dst, send_sem, recv_sem):
+        most = pl.ds(0, group - 1)
+        return pltpu.make_async_remote_copy(
+            src_ref=src(most),
+            dst_ref=dst(most),
+            send_sem=send_sem,
+            recv_sem=recv_sem,
+            device_id={"north": n, "east": e},
+            device_id_type=MESH,
+        )
+
+    def leg1(ch):
+        return (
+            lambda q: send1.at[ch, q],
+            lambda q: recv1.at[ch, q],
+            send_sem1.at[ch],
+            recv_sem1.at[ch],
+        )
+
+    tile = 4 * cols
+    parts = ((0, 0, 3), (1, 0, 3))
+
+    def leg2(i):
+        ch, start, stop = parts[i]
+        lanes = pl.ds(start * tile, (stop - start) * tile)
+        return (
+            lambda q: send2.at[ch, q, :, lanes],
+            lambda q: recv2.at[ch, q, :, lanes],
+            send_sem2.at[i],
+            recv_sem2.at[i],
+        )
+
+    for load in loads[1:]:
         load.wait()
-
+    r = iota((4 * group, width), 0)
+    d = iota((4 * group, width), 1)
+    parity = (r & 1) == 0
+
+    def spread(weights, ch):
+        picked = 0.0
+        for f, w in enumerate(weights):
+            pick = (((r >> 1) & 1) == f) & (d == (r >> 2) + ch * group)
+            picked = picked + dot_nt(jnp.where(pick, 1.0, 0.0).astype(BF16), w[...])
+        return jnp.concatenate(
+            [jnp.where(parity, picked, 0.0), jnp.where(parity, 0.0, picked)], axis=1
+        ).astype(BF16)
+
+    for ch in range(2):
+        spread_ref[2 * ch] = spread((lw_ref, rw_ref), ch)
+        spread_ref[2 * ch + 1] = spread((lg_ref, rg_ref), ch)
+
+    loads[0].wait()
     x = x_ref[...].astype(F32)
     centred = x - jnp.mean(x, axis=-1, keepdims=True)
     ready = (
@@ -119,50 +191,19 @@
     ready_ref[...] = ready
     both = jnp.concatenate([ready_ref[:lines, :], ready_ref[lines:, :]], axis=1)
 
-    def send_all(src, dst, send_sem, recv_sem):
-        dst[me] = src[me]
-        each_peer(
-            lambda pe, pn: pltpu.make_async_remote_copy(
-                src_ref=src.at[pe * north + pn],
-                dst_ref=dst.at[me],
-                send_sem=send_sem,
-                recv_sem=recv_sem,
-                device_id={"north": pn, "east": pe},
-                device_id_type=MESH,
-            ).start()
-        )
-
-    def all_of(src, dst, send_sem, recv_sem):
-        return pltpu.make_async_remote_copy(
-            src_ref=src.at[pl.ds(0, group - 1)],
-            dst_ref=dst.at[pl.ds(0, group - 1)],
-            send_sem=send_sem,
-            recv_sem=recv_sem,
-            device_id={"north": n, "east": e},
-            device_id_type=MESH,
-        )
-
-    r = iota((4 * group, width), 0)
-    d = iota((4 * group, width), 1)
-    parity = (r & 1) == 0
-
-    def spread(weights, ch):
-        picked = 0.0
-        for f, w in enumerate(weights):
-            pick = (((r >> 1) & 1) == f) & (d == (r >> 2) + ch * group)
-            picked = picked + dot_nt(jnp.where(pick, 1.0, 0.0).astype(BF16), w[...])
-        return jnp.concatenate(
-            [jnp.where(parity, picked, 0.0), jnp.where(parity, 0.0, picked)], axis=1
-        ).astype(BF16)
-
     for ch in range(2):
-        value = dot_nt(spread((lw_ref, rw_ref), ch), both)
-        gate = dot_nt(spread((lg_ref, rg_ref), ch), both)
-        value = (value * sigmoid(gate)).reshape(group, 4, lines)
-        send1[ch] = value.astype(BF16)
+        value = dot_nt(spread_ref[2 * ch], both) * sigmoid(dot_nt(spread_ref[2 * ch + 1], both))
+        send1[ch] = value.reshape(group, 4, lines).astype(BF16)
         if ch == 0:
-            pl.semaphore_wait(barrier, group - 1)
-        send_all(send1.at[ch], recv1.at[ch], send_sem1.at[ch], recv_sem1.at[ch])
+            pl.semaphore_wait(barrier, len(near))
+            for k, (dz, dy, dx) in enumerate(columns):
+                signal(known.at[k], [(0, (Y - dy) % Y, (X - dx) % X)])
+        recv1[ch, me] = send1[ch, me]
+        send(*leg1(ch), near)
+    for k, offset in sorted(enumerate(columns), key=lambda c: everyone.index(c[1]), reverse=True):
+        pl.semaphore_wait(known.at[k], 1)
+        send(*leg1(0), [o for o in rest if o[1:] == offset[1:]])
+    send(*leg1(1), rest)
 
     gate_ref[...] = sigmoid(
         jnp.dot(ready_ref[...], og_ref[...], preferred_element_type=F32)
@@ -172,7 +213,7 @@
 
     per = north // east * 2
     for ch in range(2):
-        all_of(send1.at[ch], recv1.at[ch], send_sem1.at[ch], recv_sem1.at[ch]).wait_recv()
+        all_of(*leg1(ch)).wait_recv()
         for s in range(east):
             lines_l = recv1[ch, north * s : north * (s + 1), 0:2, :].reshape(2 * north, lines)
             lines_r = recv1[ch, north * s : north * (s + 1), 2:4, :].reshape(2 * north, lines)
@@ -195,7 +236,10 @@
                 axis=1,
             )
             send2[ch, north * t : north * (t + 1)] = strip.reshape(north, 2, lines).astype(BF16)
-        send_all(send2.at[ch], recv2.at[ch], send_sem2.at[ch], recv_sem2.at[ch])
+        recv2[ch, me] = send2[ch, me]
+        for i in range(len(parts)):
+            if parts[i][0] == ch:
+                send(*leg2(i), everyone)
 
     mid_gain = jnp.broadcast_to(mid_gain_ref[...], (width, width)).T
     mid_gain = jnp.broadcast_to(mid_gain[:, None, :], (width, 2, width)).reshape(2 * width, width)
@@ -206,7 +250,6 @@
     weight = jnp.concatenate(
         [jnp.where(first, weight, 0.0), jnp.where(first, 0.0, weight)], axis=1
     ).astype(BF16)
-    tile = 4 * cols
     lane = iota((tile, tile), 1)
     block = jnp.where(lane >= 2 * cols, 2, 0)
     block = block + jnp.where(lane - block * cols >= cols, 1, 0)
@@ -214,9 +257,6 @@
     target = block * cols + ((rest & (per - 1)) >> 1) * rows + (rest & 1) * half + (rest >> 3)
     order = jnp.where(iota((tile, tile), 0) == target, 1.0, 0.0).astype(BF16)
 
-    for ch in range(2):
-        all_of(send2.at[ch], recv2.at[ch], send_sem2.at[ch], recv_sem2.at[ch]).wait_recv()
-
     def fold(total):
         total = jnp.sum(total.reshape(2 * width // 8, 8, tile), axis=0)
         total = total + pltpu.roll(total, 4, 0)
@@ -224,6 +264,9 @@
         return (total * (1.0 / width))[None]
 
     for g in range(lines // tile):
+        if g == 0:
+            all_of(*leg2(0)).wait_recv()
+            all_of(*leg2(1)).wait_recv()
         lanes = slice(g * tile, (g + 1) * tile)
         mixed = recv2[:, :, :, lanes].reshape(2 * width, tile).astype(F32)
         centred = mixed.reshape(2 * width // 8, 8, tile) - fold(mixed)
@@ -238,11 +281,9 @@
             ).astype(BF16)
 
     for ch in range(2):
-        for src, dst, a, b in (
-            (send1, recv1, send_sem1, recv_sem1),
-            (send2, recv2, send_sem2, recv_sem2),
-        ):
-            all_of(src.at[ch], dst.at[ch], a.at[ch], b.at[ch]).wait_send()
+        all_of(*leg1(ch)).wait_send()
+    for i in range(len(parts)):
+        all_of(*leg2(i)).wait_send()
 
 
 def local(
@@ -290,6 +331,8 @@
             pltpu.SemaphoreType.DMA((2,)),
             pltpu.SemaphoreType.DMA((2,)),
             pltpu.SemaphoreType.DMA((2,)),
+            pltpu.SemaphoreType.REGULAR((Y * X - 1,)),
+            pltpu.VMEM((4, 4 * group, 2 * width), BF16),
         ],
         compiler_params=pltpu.CompilerParams(
             collective_id=0, has_side_effects=True, vmem_limit_bytes=48 * 1024 * 1024

time: 56.5 us -> 53 us (0.938)
  Pallas kernels: 55.6 us -> 51.6 us
    pallas_call x1, Pallas kernels: 55.6 us -> 51.6 us  [local(): pl.pallas_call(functools.partial(kernel, north, east, rows, cols), out_sh...]
where the time goes in v6:
time: 53 us; the launch traced here: 52.4 us
  Pallas kernels  51.6 us (97%)
  local copies, waits for them, and re-layouts  0.82 us (2%)
    pallas_call x1, Pallas kernels, local(): pl.pallas_call(functools.partial(kernel, north, east, rows, cols), out_sh...  51.6 us

profile of v6, /device:TPU:8, one launch (start us, length us, event | category | flops | bytes accessed | tf_op | source)
XLA Modules:
  0.0 52.4 jit_solution(9902908693387377544)
XLA Ops:
  0.0 51.6 %shard_map.91 = bf16[2304,128]{1,0:T(8,128)(2,1)S(1)} custom-call(bf16[2304,128]{1,0:T(8,128)(2,1)} %bitcast.5, f32[1,128]{1,0:T(1,128)} %bitcast.6, bf16[128,128]{1,0:T(8,128)(2,1)} %lw_hbm.1, bf16[128,128]{1,0:T(8,128)(2,1)} %rw_hbm.1, bf16[128,128]{1,0:T(8,128)(2,1)} %lg_hbm.1, bf16[128,128]{1,0:T(8,128)(2,1)} %rg_hbm.1, f32[1,128]{1,0:T(1,128)} %bitcast.7, ...), custom_call_target="tpu_custom_call" | custom-call | tf_op jit(solution)/shard_map/pallas_call | solution.py:306
  51.6 0.8 %copy.11 = bf16[24,96,128]{2,1,0:T(8,128)(2,1)} copy(bf16[24,96,128]{2,1,0:T(8,128)(2,1)S(1)} %bitcast.4) | data formatting | bytes 1179648

commit v7 on v6

--- a/solution.py
+++ b/solution.py
@@ -64,6 +64,9 @@
     recv_sem2,
     known,
     spread_ref,
+    mixed_ref,
+    mean_ref,
+    spread0_ref,
 ):
     loads = [
         pltpu.make_async_copy(src, dst, load_sem.at[i])
@@ -162,7 +165,7 @@
             recv_sem2.at[i],
         )
 
-    for load in loads[1:]:
+    for load in loads:
         load.wait()
     r = iota((4 * group, width), 0)
     d = iota((4 * group, width), 1)
@@ -177,11 +180,6 @@
             [jnp.where(parity, picked, 0.0), jnp.where(parity, 0.0, picked)], axis=1
         ).astype(BF16)
 
-    for ch in range(2):
-        spread_ref[2 * ch] = spread((lw_ref, rw_ref), ch)
-        spread_ref[2 * ch + 1] = spread((lg_ref, rg_ref), ch)
-
-    loads[0].wait()
     x = x_ref[...].astype(F32)
     centred = x - jnp.mean(x, axis=-1, keepdims=True)
     ready = (
@@ -189,6 +187,9 @@
         * in_gain_ref[...]
     ).astype(BF16)
     ready_ref[...] = ready
+    for ch in range(2):
+        spread_ref[2 * ch] = spread((lw_ref, rw_ref), ch)
+        spread_ref[2 * ch + 1] = spread((lg_ref, rg_ref), ch)
     both = jnp.concatenate([ready_ref[:lines, :], ready_ref[lines:, :]], axis=1)
 
     for ch in range(2):
@@ -198,12 +199,13 @@
             pl.semaphore_wait(barrier, len(near))
             for k, (dz, dy, dx) in enumerate(columns):
                 signal(known.at[k], [(0, (Y - dy) % Y, (X - dx) % X)])
-        recv1[ch, me] = send1[ch, me]
         send(*leg1(ch), near)
     for k, offset in sorted(enumerate(columns), key=lambda c: everyone.index(c[1]), reverse=True):
         pl.semaphore_wait(known.at[k], 1)
         send(*leg1(0), [o for o in rest if o[1:] == offset[1:]])
     send(*leg1(1), rest)
+    for ch in range(2):
+        recv1[ch, me] = send1[ch, me]
 
     gate_ref[...] = sigmoid(
         jnp.dot(ready_ref[...], og_ref[...], preferred_element_type=F32)
@@ -236,10 +238,10 @@
                 axis=1,
             )
             send2[ch, north * t : north * (t + 1)] = strip.reshape(north, 2, lines).astype(BF16)
-        recv2[ch, me] = send2[ch, me]
         for i in range(len(parts)):
             if parts[i][0] == ch:
                 send(*leg2(i), everyone)
+        recv2[ch, me] = send2[ch, me]
 
     mid_gain = jnp.broadcast_to(mid_gain_ref[...], (width, width)).T
     mid_gain = jnp.broadcast_to(mid_gain[:, None, :], (width, 2, width)).reshape(2 * width, width)
@@ -258,20 +260,42 @@
     order = jnp.where(iota((tile, tile), 0) == target, 1.0, 0.0).astype(BF16)
 
     def fold(total):
-        total = jnp.sum(total.reshape(2 * width // 8, 8, tile), axis=0)
+        total = jnp.sum(total.reshape(width // 8, 8, lines), axis=0)
         total = total + pltpu.roll(total, 4, 0)
-        total = total + pltpu.roll(total, 2, 0)
-        return (total * (1.0 / width))[None]
+        return (total + pltpu.roll(total, 2, 0)) * (2.0 / width)
+
+    def centre(values, middle):
+        return (values.reshape(width // 8, 8, lines) - middle[None]).reshape(width, lines)
+
+    all_of(*leg2(0)).wait_recv()
+    mixed = recv2[0].reshape(width, lines).astype(F32)
+    mean0 = fold(mixed)
+    mixed = centre(mixed, mean0)
+    mixed_ref[...] = mixed
+    mean_ref[...] = mean0
+    spread0_ref[...] = fold(mixed * mixed)
+    all_of(*leg2(1)).wait_recv()
+    mixed = recv2[1].reshape(width, lines).astype(F32)
+    mean1 = fold(mixed)
+    mixed = centre(mixed, mean1)
+    step = 0.5 * (mean1 - mean_ref[...])
+    variance = 0.5 * (fold(mixed * mixed) + spread0_ref[...]) + step * step
+    scale = lax.rsqrt(variance + EPS)
 
     for g in range(lines // tile):
-        if g == 0:
-            all_of(*leg2(0)).wait_recv()
-            all_of(*leg2(1)).wait_recv()
         lanes = slice(g * tile, (g + 1) * tile)
-        mixed = recv2[:, :, :, lanes].reshape(2 * width, tile).astype(F32)
-        centred = mixed.reshape(2 * width // 8, 8, tile) - fold(mixed)
-        scale = lax.rsqrt(fold((centred * centred).reshape(2 * width, tile)) + EPS)
-        scaled = ((centred * scale).reshape(2 * width, tile) * mid_gain).astype(BF16)
+
+        def finish(values, shift, gain):
+            values = values.reshape(width // 8, 8, tile) + shift[None, :, lanes]
+            return ((values * scale[None, :, lanes]).reshape(width, tile) * gain).astype(BF16)
+
+        scaled = jnp.concatenate(
+            [
+                finish(mixed_ref[:, lanes], -step, mid_gain[:width]),
+                finish(mixed[:, lanes], step, mid_gain[width:]),
+            ],
+            axis=0,
+        )
         turned = dot_nt(order, scaled).astype(BF16)
         result = jnp.dot(turned, weight, preferred_element_type=F32)
         for h in range(2):
@@ -333,6 +357,9 @@
             pltpu.SemaphoreType.DMA((2,)),
             pltpu.SemaphoreType.REGULAR((Y * X - 1,)),
             pltpu.VMEM((4, 4 * group, 2 * width), BF16),
+            pltpu.VMEM((width, lines), F32),
+            pltpu.VMEM((8, lines), F32),
+            pltpu.VMEM((8, lines), F32),
         ],
         compiler_params=pltpu.CompilerParams(
             collective_id=0, has_side_effects=True, vmem_limit_bytes=48 * 1024 * 1024

time: 53 us -> 52.7 us (level)
  no operation moved by 1% of the time
where the time goes in v7:
time: 52.7 us; the launch traced here: 52.1 us
  Pallas kernels  51.3 us (97%)
  local copies, waits for them, and re-layouts  0.82 us (2%)
    pallas_call x1, Pallas kernels, local(): pl.pallas_call(functools.partial(kernel, north, east, rows, cols), out_sh...  51.3 us

profile of v7, /device:TPU:8, one launch (start us, length us, event | category | flops | bytes accessed | tf_op | source)
XLA Modules:
  0.0 52.1 jit_solution(1626160950179602095)
XLA Ops:
  0.0 51.3 %shard_map.91 = bf16[2304,128]{1,0:T(8,128)(2,1)S(1)} custom-call(bf16[2304,128]{1,0:T(8,128)(2,1)} %bitcast.5, f32[1,128]{1,0:T(1,128)} %bitcast.6, bf16[128,128]{1,0:T(8,128)(2,1)} %lw_hbm.1, bf16[128,128]{1,0:T(8,128)(2,1)} %rw_hbm.1, bf16[128,128]{1,0:T(8,128)(2,1)} %lg_hbm.1, bf16[128,128]{1,0:T(8,128)(2,1)} %rg_hbm.1, f32[1,128]{1,0:T(1,128)} %bitcast.7, ...), custom_call_target="tpu_custom_call" | custom-call | tf_op jit(solution)/shard_map/pallas_call | solution.py:330
  51.3 0.8 %copy.11 = bf16[24,96,128]{2,1,0:T(8,128)(2,1)} copy(bf16[24,96,128]{2,1,0:T(8,128)(2,1)S(1)} %bitcast.4) | data formatting | bytes 1179648

commit v8 on v7

--- a/solution.py
+++ b/solution.py
@@ -67,6 +67,7 @@
     mixed_ref,
     mean_ref,
     spread0_ref,
+    strip_ref,
 ):
     loads = [
         pltpu.make_async_copy(src, dst, load_sem.at[i])
@@ -180,26 +181,34 @@
             [jnp.where(parity, picked, 0.0), jnp.where(parity, 0.0, picked)], axis=1
         ).astype(BF16)
 
-    x = x_ref[...].astype(F32)
-    centred = x - jnp.mean(x, axis=-1, keepdims=True)
-    ready = (
-        centred * lax.rsqrt(jnp.mean(centred * centred, axis=-1, keepdims=True) + EPS)
-        * in_gain_ref[...]
-    ).astype(BF16)
-    ready_ref[...] = ready
+    for c in range(0, 2 * lines, 128):
+        some = slice(c, c + 128)
+        x = x_ref[some, :].astype(F32)
+        centred = x - jnp.mean(x, axis=-1, keepdims=True)
+        ready_ref[some, :] = (
+            centred
+            * lax.rsqrt(jnp.mean(centred * centred, axis=-1, keepdims=True) + EPS)
+            * in_gain_ref[...]
+        ).astype(BF16)
     for ch in range(2):
         spread_ref[2 * ch] = spread((lw_ref, rw_ref), ch)
         spread_ref[2 * ch + 1] = spread((lg_ref, rg_ref), ch)
     both = jnp.concatenate([ready_ref[:lines, :], ready_ref[lines:, :]], axis=1)
 
     for ch in range(2):
-        value = dot_nt(spread_ref[2 * ch], both) * sigmoid(dot_nt(spread_ref[2 * ch + 1], both))
-        send1[ch] = value.reshape(group, 4, lines).astype(BF16)
+        for g in range(0, lines, tile):
+            some = both[g : g + tile, :]
+            value = dot_nt(spread_ref[2 * ch], some) * sigmoid(dot_nt(spread_ref[2 * ch + 1], some))
+            send1[ch, :, :, g : g + tile] = value.reshape(group, 4, tile).astype(BF16)
         if ch == 0:
             pl.semaphore_wait(barrier, len(near))
             for k, (dz, dy, dx) in enumerate(columns):
                 signal(known.at[k], [(0, (Y - dy) % Y, (X - dx) % X)])
-        send(*leg1(ch), near)
+
+        @pl.when(at_z >= 0)
+        def _(ch=ch):
+            send(*leg1(ch), near)
+
     for k, offset in sorted(enumerate(columns), key=lambda c: everyone.index(c[1]), reverse=True):
         pl.semaphore_wait(known.at[k], 1)
         send(*leg1(0), [o for o in rest if o[1:] == offset[1:]])
@@ -214,6 +223,13 @@
     right_ref[...] = jnp.zeros_like(right_ref)
 
     per = north // east * 2
+    lane = iota((tile, tile), 1)
+    block = jnp.where(lane >= 2 * cols, 2, 0)
+    block = block + jnp.where(lane - block * cols >= cols, 1, 0)
+    rest = lane - block * cols
+    target = block * cols + ((rest & (per - 1)) >> 1) * rows + (rest & 1) * half + (rest >> 3)
+    order = jnp.where(iota((tile, tile), 0) == target, 1.0, 0.0).astype(BF16)
+
     for ch in range(2):
         all_of(*leg1(ch)).wait_recv()
         for s in range(east):
@@ -237,7 +253,11 @@
                 ],
                 axis=1,
             )
-            send2[ch, north * t : north * (t + 1)] = strip.reshape(north, 2, lines).astype(BF16)
+            strip_ref[2 * north * t : 2 * north * (t + 1), :] = strip.astype(BF16)
+        for g in range(lines // tile):
+            lanes = slice(g * tile, (g + 1) * tile)
+            strip = dot_nt(strip_ref[:, lanes], order)
+            send2[ch, :, :, lanes] = strip.reshape(group, 2, tile).astype(BF16)
         for i in range(len(parts)):
             if parts[i][0] == ch:
                 send(*leg2(i), everyone)
@@ -252,52 +272,46 @@
     weight = jnp.concatenate(
         [jnp.where(first, weight, 0.0), jnp.where(first, 0.0, weight)], axis=1
     ).astype(BF16)
-    lane = iota((tile, tile), 1)
-    block = jnp.where(lane >= 2 * cols, 2, 0)
-    block = block + jnp.where(lane - block * cols >= cols, 1, 0)
-    rest = lane - block * cols
-    target = block * cols + ((rest & (per - 1)) >> 1) * rows + (rest & 1) * half + (rest >> 3)
-    order = jnp.where(iota((tile, tile), 0) == target, 1.0, 0.0).astype(BF16)
-
     def fold(total):
-        total = jnp.sum(total.reshape(width // 8, 8, lines), axis=0)
+        total = jnp.sum(total, axis=0)
         total = total + pltpu.roll(total, 4, 0)
         return (total + pltpu.roll(total, 2, 0)) * (2.0 / width)
 
-    def centre(values, middle):
-        return (values.reshape(width // 8, 8, lines) - middle[None]).reshape(width, lines)
-
+    def take(ch, lanes):
+        values = recv2[ch, :, :, lanes].reshape(width, tile).astype(F32)
+        values = values.reshape(width // 8, 8, tile)
+        mean = fold(values)
+        values = values - mean[None]
+        return values, mean, fold(values * values)
+
+    tiles = [slice(g * tile, (g + 1) * tile) for g in range(lines // tile)]
     all_of(*leg2(0)).wait_recv()
-    mixed = recv2[0].reshape(width, lines).astype(F32)
-    mean0 = fold(mixed)
-    mixed = centre(mixed, mean0)
-    mixed_ref[...] = mixed
-    mean_ref[...] = mean0
-    spread0_ref[...] = fold(mixed * mixed)
+    for lanes in tiles:
+        values, mean_ref[:, lanes], spread0_ref[:, lanes] = take(0, lanes)
+        mixed_ref[:, lanes] = values.reshape(width, tile)
     all_of(*leg2(1)).wait_recv()
-    mixed = recv2[1].reshape(width, lines).astype(F32)
-    mean1 = fold(mixed)
-    mixed = centre(mixed, mean1)
-    step = 0.5 * (mean1 - mean_ref[...])
-    variance = 0.5 * (fold(mixed * mixed) + spread0_ref[...]) + step * step
-    scale = lax.rsqrt(variance + EPS)
-
-    for g in range(lines // tile):
-        lanes = slice(g * tile, (g + 1) * tile)
+    for g, lanes in enumerate(tiles):
+        values, mean, variance = take(1, lanes)
+        step = 0.5 * (mean - mean_ref[:, lanes])
+        variance = 0.5 * (variance + spread0_ref[:, lanes]) + step * step
+        scale = lax.rsqrt(variance + EPS)
 
         def finish(values, shift, gain):
-            values = values.reshape(width // 8, 8, tile) + shift[None, :, lanes]
-            return ((values * scale[None, :, lanes]).reshape(width, tile) * gain).astype(BF16)
+            values = (values + shift[None]) * scale[None]
+            return (values.reshape(width, tile) * gain).astype(BF16)
 
         scaled = jnp.concatenate(
             [
-                finish(mixed_ref[:, lanes], -step, mid_gain[:width]),
-                finish(mixed[:, lanes], step, mid_gain[width:]),
+                finish(
+                    mixed_ref[:, lanes].reshape(width // 8, 8, tile), -step, mid_gain[:width]
+                ),
+                finish(values, step, mid_gain[width:]),
             ],
             axis=0,
         )
-        turned = dot_nt(order, scaled).astype(BF16)
-        result = jnp.dot(turned, weight, preferred_element_type=F32)
+        result = lax.dot_general(
+            scaled, weight, (((0,), (0,)), ((), ())), preferred_element_type=F32
+        )
         for h in range(2):
             at = slice(h * lines + g * tile, h * lines + (g + 1) * tile)
             out_ref[at, :] = (
@@ -360,6 +374,7 @@
             pltpu.VMEM((width, lines), F32),
             pltpu.VMEM((8, lines), F32),
             pltpu.VMEM((8, lines), F32),
+            pltpu.VMEM((2 * group, lines), BF16),
         ],
         compiler_params=pltpu.CompilerParams(
             collective_id=0, has_side_effects=True, vmem_limit_bytes=48 * 1024 * 1024

time: 52.7 us -> 52.2 us (level)
  Pallas kernels: 51.3 us -> 50.7 us
    pallas_call x1, Pallas kernels: 51.3 us -> 50.7 us  [local(): pl.pallas_call(functools.partial(kernel, north, east, rows, cols), out_sh...]
where the time goes in v8:
time: 52.2 us; the launch traced here: 51.6 us
  Pallas kernels  50.7 us (97%)
  local copies, waits for them, and re-layouts  0.82 us (2%)
    pallas_call x1, Pallas kernels, local(): pl.pallas_call(functools.partial(kernel, north, east, rows, cols), out_sh...  50.7 us

profile of v8, /device:TPU:8, one launch (start us, length us, event | category | flops | bytes accessed | tf_op | source)
XLA Modules:
  0.0 51.6 jit_solution(4476001617891099411)
XLA Ops:
  0.0 50.7 %shard_map.91 = bf16[2304,128]{1,0:T(8,128)(2,1)S(1)} custom-call(bf16[2304,128]{1,0:T(8,128)(2,1)} %bitcast.5, f32[1,128]{1,0:T(1,128)} %bitcast.6, bf16[128,128]{1,0:T(8,128)(2,1)} %lw_hbm.1, bf16[128,128]{1,0:T(8,128)(2,1)} %rw_hbm.1, bf16[128,128]{1,0:T(8,128)(2,1)} %lg_hbm.1, bf16[128,128]{1,0:T(8,128)(2,1)} %rg_hbm.1, f32[1,128]{1,0:T(1,128)} %bitcast.7, ...), custom_call_target="tpu_custom_call" | custom-call | tf_op jit(solution)/shard_map/pallas_call | solution.py:344
  50.8 0.8 %copy.11 = bf16[24,96,128]{2,1,0:T(8,128)(2,1)} copy(bf16[24,96,128]{2,1,0:T(8,128)(2,1)S(1)} %bitcast.4) | data formatting | bytes 1179648

commit v9 on v8

--- a/solution.py
+++ b/solution.py
@@ -200,15 +200,11 @@
             some = both[g : g + tile, :]
             value = dot_nt(spread_ref[2 * ch], some) * sigmoid(dot_nt(spread_ref[2 * ch + 1], some))
             send1[ch, :, :, g : g + tile] = value.reshape(group, 4, tile).astype(BF16)
-        if ch == 0:
-            pl.semaphore_wait(barrier, len(near))
-            for k, (dz, dy, dx) in enumerate(columns):
-                signal(known.at[k], [(0, (Y - dy) % Y, (X - dx) % X)])
-
-        @pl.when(at_z >= 0)
-        def _(ch=ch):
-            send(*leg1(ch), near)
-
+    pl.semaphore_wait(barrier, len(near))
+    for k, (dz, dy, dx) in enumerate(columns):
+        signal(known.at[k], [(0, (Y - dy) % Y, (X - dx) % X)])
+    send(*leg1(0), near)
+    send(*leg1(1), near)
     for k, offset in sorted(enumerate(columns), key=lambda c: everyone.index(c[1]), reverse=True):
         pl.semaphore_wait(known.at[k], 1)
         send(*leg1(0), [o for o in rest if o[1:] == offset[1:]])

time: 52.2 us -> 51.9 us (level)
  no operation moved by 1% of the time
where the time goes in v9:
time: 51.9 us; the launch traced here: 51.4 us
  Pallas kernels  50.6 us (97%)
  local copies, waits for them, and re-layouts  0.82 us (2%)
    pallas_call x1, Pallas kernels, local(): pl.pallas_call(functools.partial(kernel, north, east, rows, cols), out_sh...  50.6 us

profile of v9, /device:TPU:8, one launch (start us, length us, event | category | flops | bytes accessed | tf_op | source)
XLA Modules:
  0.0 51.4 jit_solution(5716495911222364600)
XLA Ops:
  0.0 50.6 %shard_map.91 = bf16[2304,128]{1,0:T(8,128)(2,1)S(1)} custom-call(bf16[2304,128]{1,0:T(8,128)(2,1)} %bitcast.5, f32[1,128]{1,0:T(1,128)} %bitcast.6, bf16[128,128]{1,0:T(8,128)(2,1)} %lw_hbm.1, bf16[128,128]{1,0:T(8,128)(2,1)} %rw_hbm.1, bf16[128,128]{1,0:T(8,128)(2,1)} %lg_hbm.1, bf16[128,128]{1,0:T(8,128)(2,1)} %rg_hbm.1, f32[1,128]{1,0:T(1,128)} %bitcast.7, ...), custom_call_target="tpu_custom_call" | custom-call | tf_op jit(solution)/shard_map/pallas_call | solution.py:340
  50.6 0.8 %copy.11 = bf16[24,96,128]{2,1,0:T(8,128)(2,1)} copy(bf16[24,96,128]{2,1,0:T(8,128)(2,1)S(1)} %bitcast.4) | data formatting | bytes 1179648
